TPU v7x, 32 devices: a whole 2x2x4 slice. The times are simulated.
32 devices in a mesh: mkt: 4 (over z), draw: 4 (over y, core), nest: 2 (over x).
Axes of the slice: x: 2, y: 2, z: 4, core: 2. Of those that a mesh axis runs over, the one named last changes fastest.
Arguments:
- features: bfloat16 [32, 512, 128], P(None, 'mkt'), may hold values from -1.5 to 1.5
- taste_draws: bfloat16 [128, 32, 512], P('mkt', None, 'draw'), may hold values from -4 to 4
- taste_scale: float32 [32], replicated, may hold values from 0.2 to 1
- nest_param: float32 [16], P('nest'), may hold values from 0.3 to 0.95
- members: int32 [16, 48], P('nest'), may hold values from -1 to 511, as said below
- log_share: float32 [512, 128], P('mkt'), may hold values from -10 to -7
Outputs:
- mean_utility: float32 [128, 768], P('mkt', 'nest')
- model_share: float32 [128, 768], P('mkt', 'nest')
Inputs may be any that keep to these rules, and one draw needn't show every extreme that they name: `members`: every product id 0 to 511 stands in exactly one slot; in each nest's row the ids fill the first slots and -1 fills the rest; each nest holds at least 16 products, and some nest fills all 48 slots.
All inputs are finite; a program needn't handle non-finite values.
Results may differ from a plain program's by a relative error of at most 0.0013.
The roundings to bfloat16 on the way count: a program that leaves them out, or rounds other values in their place, can miss the bound.
Values may be sent and summed in bfloat16 or wider, within the bound.
A program may use at most 64 MiB of HBM per device.

v0:
```python
import jax
import jax.numpy as jnp
from jax import lax
from jax.sharding import PartitionSpec as P

ITERS = 3


def revise(value_slot, slot_share, target, nest_rate, occupied):
    safe_share = jnp.where(occupied[None, :], slot_share, 1.0)
    moved_value = value_slot + (1.0 - nest_rate)[None, :] * (target - jnp.log(safe_share))
    return jnp.where(occupied[None, :], moved_value, 0.0)


def shards(features, taste_draws, taste_scale, nest_param, members, log_share):
    market_x = lax.all_to_all(features, "mkt", split_axis=2, concat_axis=1, tiled=True)
    market_log = lax.all_to_all(log_share, "mkt", split_axis=1, concat_axis=0, tiled=True)
    market_list = market_log.shape[1]
    product_count = market_log.shape[0]
    nest_count = members.shape[0]
    slot_count = members.shape[1]
    columns = nest_count * slot_count
    draws_here = taste_draws.shape[2]
    total_draws = draws_here * lax.axis_size("draw")
    product_ids = members.reshape(columns)
    occupied = product_ids >= 0
    safe_ids = jnp.maximum(product_ids, 0)
    live_flag = occupied.astype(jnp.float32)
    product_range = jnp.arange(product_count, dtype=jnp.int32)
    onehot = ((safe_ids[None, :] == product_range[:, None]) & occupied[None, :]).astype(
        jnp.bfloat16
    )
    slot_features = jnp.einsum(
        "kjm,js->mks", market_x, onehot, preferred_element_type=jnp.float32
    ).astype(jnp.bfloat16)
    slot_log = jnp.transpose(jnp.take(market_log, safe_ids, axis=0), (1, 0))
    outside = 1.0 - jnp.sum(jnp.exp(market_log), axis=0)
    value_slot = jnp.where(occupied[None, :], slot_log - jnp.log(outside)[:, None], 0.0)
    taste_matrix = (taste_scale[None, :, None] * taste_draws.astype(jnp.float32)).astype(
        jnp.bfloat16
    )
    nest_rate = jnp.repeat(nest_param, slot_count)
    mean_utility_part = jnp.einsum(
        "dve,dvb->deb", slot_features, taste_matrix, preferred_element_type=jnp.float32
    )
    slot_share = jnp.zeros_like(value_slot)
    for iteration in range(ITERS):
        utility = live_flag[None, :, None] * jnp.exp(
            (value_slot[:, :, None] + mean_utility_part) / nest_rate[None, :, None]
        )
        grouped = utility.reshape(market_list, nest_count, slot_count, draws_here)
        inner_sum = jnp.sum(grouped, axis=2)
        inclusive_value = jnp.exp(nest_param[None, :, None] * jnp.log(inner_sum))
        totals = lax.psum(jnp.sum(inclusive_value, axis=1), "nest")
        nest_ratio = inclusive_value / (inner_sum * (1.0 + totals)[:, None, :])
        share_terms = jnp.sum(grouped * nest_ratio[:, :, None, :], axis=3).reshape(
            market_list, columns
        )
        slot_share = lax.psum(share_terms, "draw") / total_draws
        value_slot = revise(value_slot, slot_share, slot_log, nest_rate, occupied)
    return (value_slot, slot_share)


def solution(mesh):
    in_specs = (
        P(None, "mkt", None),
        P("mkt", None, "draw"),
        P(),
        P("nest"),
        P("nest", None),
        P("mkt", None),
    )
    out_specs = (P("mkt", "nest"), P("mkt", "nest"))
    return jax.shard_map(shards, mesh=mesh, in_specs=in_specs, out_specs=out_specs, check_vma=False)
```

profile of v0, /device:TPU:1, one launch (start us, length us, event | category | flops | bytes accessed | tf_op | source)
XLA Modules:
  0.0 170.8 jit_solution(5884183083681372627)
XLA Ops:
  0.7 1.6 copy.23
  2.2 5.4 %all-to-all-start = ((f32[128,4,32]{0,2,1:T(8,128)}), f32[128,4,32]{0,2,1:T(8,128)S(1)}, u32[]{:S(2)}, u32[]{:S(2)}) async-start(f32[128,4,32]{0,2,1:T(8,128)} %bitcast), calls=%async_computation | async-start | bytes 131072 | tf_op jit(solution)/shard_map/all_to_all | solution.py:17
  7.7 0.7 broadcast_in_dim.85
  8.5 2.7 %copy.26 = bf16[32,128,128]{1,0,2:T(8,128)(2,1)} copy(bf16[32,128,128]{2,1,0:T(8,128)(2,1)} %param.6) | data formatting | bytes 2097152 | tf_op args[0]
  11.2 1.1 all-to-all-done
  12.3 3.5 %all-to-all-start.1 = ((bf16[32,128,128]{1,0,2:T(8,128)(2,1)}), bf16[32,128,128]{1,0,2:T(8,128)(2,1)S(1)}, u32[]{:S(2)}, u32[]{:S(2)}) async-start(bf16[32,128,128]{1,0,2:T(8,128)(2,1)} %copy.26), calls=%async_computation.1 | async-start | bytes 2097152 | tf_op jit(solution)/shard_map/all_to_all | solution.py:16
  15.8 0.7 broadcast_maximum_fusion
  16.5 0.7 broadcast_compare_fusion
  17.5 1.1 gather_fusion
  19.1 22.0 %all-to-all-done.1 = bf16[32,128,128]{1,0,2:T(8,128)(2,1)S(1)} async-done(((bf16[32,128,128]{1,0,2:T(8,128)(2,1)}), bf16[32,128,128]{1,0,2:T(8,128)(2,1)S(1)}, u32[]{:S(2)}, u32[]{:S(2)}) %all-to-all-start.1) | async-done | bytes 1048608 | tf_op jit(solution)/shard_map/all_to_all | solution.py:16
  41.0 6.5 %exponential_multiply_fusion.2 = (f32[32,384,128]{2,1,0:T(8,128)}, f32[32,384,128]{2,1,0:T(8,128)}) fusion(f32[384]{0:T(512)S(1)} %reshape.109, f32[32,384]{1,0:T(8,128)S(1)} %copy.25, f32[384]{0:T(512)S(1)} %convert_element_type.20, bf16[32,32,128]{2,1,0:T(8,128)(2,1)S(1)} %copy-done.1, f32[32]{0:T(128)S(1)} %copy-done.2, ...), kind=kOutput, calls=%fused_computation.6 | convolution fusion | flops 509214720 | bytes 13947904 | tf_op jit(solution)/shard_map/dve,dvb->deb/dot_general | solution.py:43
  47.5 3.7 %reduce_sum.91 = f32[32,8,128]{2,1,0:T(8,128)S(1)} reduce(f32[32,8,48,128]{3,2,1,0:T(8,128)} %bitcast.62, f32[]{:T(128)} %constant.28.clone.1), dimensions={2}, to_apply=%region_1.2 | reduce | flops 1540096 | bytes 6422532 | tf_op jit(solution)/shard_map/reduce_sum | solution.py:52
  51.3 6.1 %psum.42 = f32[32,128]{1,0:T(8,128)S(1)} all-reduce(f32[32,128]{1,0:T(8,128)S(1)} %fusion.27), channel_id=1, replica_groups=mesh['mkt'=4,'draw'=4,'nest'=2] {'nest'}, use_global_device_ids=true, to_apply=%region_3.4 | all-reduce | flops 4096 | bytes 32768 | tf_op jit(solution)/shard_map/psum | solution.py:54
  57.5 6.2 %bitcast_multiply_fusion.2 = f32[32,384,128]{2,1,0:T(8,128)} fusion(f32[32,384,128]{2,1,0:T(8,128)} %get-tuple-element.10, f32[32,8,128]{2,1,0:T(8,128)S(1)} %multiply_divide_fusion.2), kind=kLoop, calls=%fused_computation.3 | loop fusion | flops 1572864 | bytes 12713984 | tf_op jit(solution)/shard_map/mul | solution.py:56
  63.8 4.5 %reduce_sum.93 = f32[32,384]{1,0:T(8,128)S(1)} reduce(f32[32,384,128]{2,1,0:T(8,128)} %bitcast_multiply_fusion.2, f32[]{:T(128)} %constant.28.clone.1), dimensions={2}, to_apply=%region_4.5 | reduce | flops 1560576 | bytes 6340612 | tf_op jit(solution)/shard_map/reduce_sum | solution.py:56
  68.4 15.4 %psum.43 = f32[32,384]{0,1:T(8,128)S(1)} all-reduce(f32[32,384]{0,1:T(8,128)S(1)} %copy.30), channel_id=1, replica_groups=mesh['mkt'=4,'draw'=4,'nest'=2] {'draw'}, use_global_device_ids=true, to_apply=%region_5.6 | all-reduce | flops 12288 | bytes 98304 | tf_op jit(solution)/shard_map/psum | solution.py:59
  84.1 6.8 %exponential_multiply_fusion.1 = f32[32,384,128]{2,1,0:T(8,128)} fusion(f32[32,384,128]{2,1,0:T(8,128)} %get-tuple-element.11, f32[32,384]{1,0:T(8,128)S(1)} %copy.31, f32[384]{0:T(512)S(1)} %reshape.109, f32[384]{0:T(512)S(1)} %convert_element_type.20), kind=kLoop, calls=%fused_computation.5 | loop fusion | flops 4718592 | bytes 12635136 | tf_op jit(solution)/shard_map/mul | solution.py:48
  90.9 3.7 %reduce_sum.94 = f32[32,8,128]{2,1,0:T(8,128)S(1)} reduce(f32[32,8,48,128]{3,2,1,0:T(8,128)} %bitcast.63, f32[]{:T(128)} %constant.28.clone.1), dimensions={2}, to_apply=%region_6.7 | reduce | flops 1540096 | bytes 6422532 | tf_op jit(solution)/shard_map/reduce_sum | solution.py:52
  94.6 5.2 %psum.44 = f32[32,128]{1,0:T(8,128)S(1)} all-reduce(f32[32,128]{1,0:T(8,128)S(1)} %fusion.26), channel_id=1, replica_groups=mesh['mkt'=4,'draw'=4,'nest'=2] {'nest'}, use_global_device_ids=true, to_apply=%region_8.9 | all-reduce | flops 4096 | bytes 32768 | tf_op jit(solution)/shard_map/psum | solution.py:54
  99.9 6.9 %bitcast_multiply_fusion.1 = f32[32,384,128]{2,1,0:T(8,128)} fusion(f32[32,8,128]{2,1,0:T(8,128)S(1)} %multiply_divide_fusion.1, f32[384]{0:T(512)S(1)} %reshape.109, f32[32,384,128]{2,1,0:T(8,128)} %get-tuple-element.11, f32[32,384]{1,0:T(8,128)S(1)} %copy.31, f32[384]{0:T(512)S(1)} %convert_element_type.20), kind=kLoop, calls=%fused_computation.2 | loop fusion | flops 6291456 | bytes 12766208 | tf_op jit(solution)/shard_map/mul | solution.py:56
  106.9 4.5 %reduce_sum.96 = f32[32,384]{1,0:T(8,128)S(1)} reduce(f32[32,384,128]{2,1,0:T(8,128)} %bitcast_multiply_fusion.1, f32[]{:T(128)} %constant.28.clone.1), dimensions={2}, to_apply=%region_9.10 | reduce | flops 1560576 | bytes 6340612 | tf_op jit(solution)/shard_map/reduce_sum | solution.py:56
  111.5 14.6 %psum.45 = f32[32,384]{0,1:T(8,128)S(1)} all-reduce(f32[32,384]{0,1:T(8,128)S(1)} %copy.32), channel_id=1, replica_groups=mesh['mkt'=4,'draw'=4,'nest'=2] {'draw'}, use_global_device_ids=true, to_apply=%region_10.11 | all-reduce | flops 12288 | bytes 98304 | tf_op jit(solution)/shard_map/psum | solution.py:59
  126.1 0.2 fusion.21
  126.4 6.8 %exponential_multiply_fusion = f32[32,384,128]{2,1,0:T(8,128)} fusion(f32[32,384,128]{2,1,0:T(8,128)} %get-tuple-element.11, f32[32,384]{1,0:T(8,128)S(1)} %copy.33, f32[384]{0:T(512)S(1)} %reshape.109, f32[384]{0:T(512)S(1)} %convert_element_type.20), kind=kLoop, calls=%fused_computation.4 | loop fusion | flops 4718592 | bytes 12635136 | tf_op jit(solution)/shard_map/mul | solution.py:48
  133.2 3.7 %reduce_sum.97 = f32[32,8,128]{2,1,0:T(8,128)S(1)} reduce(f32[32,8,48,128]{3,2,1,0:T(8,128)} %bitcast.64, f32[]{:T(128)} %constant.28.clone.1), dimensions={2}, to_apply=%region_11.12 | reduce | flops 1540096 | bytes 6422532 | tf_op jit(solution)/shard_map/reduce_sum | solution.py:52
  137.0 6.1 %psum.46 = f32[32,128]{1,0:T(8,128)S(1)} all-reduce(f32[32,128]{1,0:T(8,128)S(1)} %fusion.25), channel_id=1, replica_groups=mesh['mkt'=4,'draw'=4,'nest'=2] {'nest'}, use_global_device_ids=true, to_apply=%region_13.14 | all-reduce | flops 4096 | bytes 32768 | tf_op jit(solution)/shard_map/psum | solution.py:54
  143.2 6.9 %bitcast_multiply_fusion = f32[32,384,128]{2,1,0:T(8,128)} fusion(f32[32,8,128]{2,1,0:T(8,128)S(1)} %multiply_divide_fusion, f32[384]{0:T(512)S(1)} %reshape.109, f32[32,384,128]{2,1,0:T(8,128)} %get-tuple-element.11, f32[32,384]{1,0:T(8,128)S(1)} %copy.33, f32[384]{0:T(512)S(1)} %convert_element_type.20), kind=kLoop, calls=%fused_computation.1 | loop fusion | flops 6291456 | bytes 12766208 | tf_op jit(solution)/shard_map/mul | solution.py:56
  150.1 4.5 %reduce_sum.99 = f32[32,384]{1,0:T(8,128)S(1)} reduce(f32[32,384,128]{2,1,0:T(8,128)} %bitcast_multiply_fusion, f32[]{:T(128)} %constant.28.clone.1), dimensions={2}, to_apply=%region_14.15 | reduce | flops 1560576 | bytes 6340612 | tf_op jit(solution)/shard_map/reduce_sum | solution.py:56
  154.7 14.4 %psum.47 = f32[32,384]{0,1:T(8,128)S(1)} all-reduce(f32[32,384]{0,1:T(8,128)S(1)} %copy.34), channel_id=1, replica_groups=mesh['mkt'=4,'draw'=4,'nest'=2] {'draw'}, use_global_device_ids=true, to_apply=%region_15.16 | all-reduce | flops 12288 | bytes 98304 | tf_op jit(solution)/shard_map/psum | solution.py:59
  169.1 0.2 broadcast_multiply_fusion
  169.4 0.7 copy.35
  170.1 0.7 copy.36
  (33 shorter events, 2.3 us)
Async XLA Ops:
  0.6 40.4 %copy-start.1 = (bf16[32,32,128]{2,1,0:T(8,128)(2,1)S(1)}, bf16[32,32,128]{2,1,0:T(8,128)(2,1)}, u32[]{:S(2)}) copy-start(bf16[32,32,128]{2,1,0:T(8,128)(2,1)} %param.7) | copy-start | bytes 786436
  0.6 40.4 %copy-start.2 = (f32[32]{0:T(128)S(1)}, f32[32]{0:T(128)}, u32[]{:S(2)}) copy-start(f32[32]{0:T(128)} %param.8) | copy-start | bytes 388
  2.2 10.0 %all-to-all-start = ((f32[128,4,32]{0,2,1:T(8,128)}), f32[128,4,32]{0,2,1:T(8,128)S(1)}, u32[]{:S(2)}, u32[]{:S(2)}) async-start(f32[128,4,32]{0,2,1:T(8,128)} %bitcast), calls=%async_computation | async-start | bytes 131072 | tf_op jit(solution)/shard_map/all_to_all | solution.py:17
  12.3 28.8 %all-to-all-start.1 = ((bf16[32,128,128]{1,0,2:T(8,128)(2,1)}), bf16[32,128,128]{1,0,2:T(8,128)(2,1)S(1)}, u32[]{:S(2)}, u32[]{:S(2)}) async-start(bf16[32,128,128]{1,0,2:T(8,128)(2,1)} %copy.26), calls=%async_computation.1 | async-start | bytes 2097152 | tf_op jit(solution)/shard_map/all_to_all | solution.py:16
  47.5 3.7 %copy-start = (f32[8]{0:T(128)S(1)}, f32[8]{0:T(128)}, u32[]{:S(2)}) copy-start(f32[8]{0:T(128)} %param.9) | copy-start | bytes 100
where the time goes:
time: 172 us; the launch traced here: 171 us
  blocking collectives  61.8 us (36%)
  other arithmetic  61.1 us (36%)
  waiting for transfers between devices  23.1 us (13%)
  starting transfers between devices  8.92 us (5%)
  local copies, waits for them, and re-layouts  8.63 us (5%)
  matrix products  6.48 us (4%)
    psum x3, blocking collectives, shards(): slot_share = lax.psum(share_terms, 'draw') / total_draws  44.3 us
    all_to_all x1, waiting for transfers between devices, shards(): lax.all_to_all(features, 'mkt', split_axis=2, concat_axis=1, tiled=True)  22 us
    mul x3, other arithmetic, shards(): grouped * nest_ratio[:, :, None, :]  20.1 us
    psum x3, blocking collectives, shards(): totals = lax.psum(jnp.sum(inclusive_value, axis=1), 'nest')  17.4 us
    mul x2, other arithmetic, shards(): live_flag[None, :, None]  13.6 us
    reduce_sum x3, other arithmetic, shards(): jnp.sum(grouped * nest_ratio[:, :, None, :], axis=3)  13.4 us
    reduce_sum x3, other arithmetic, shards(): inner_sum = jnp.sum(grouped, axis=2)  11 us
    dot_general x1, matrix products, shards(): jnp.einsum('dve,dvb->deb', slot_features, taste_matrix, preferred_element...  6.48 us
  transfers between devices with their start and end apart: 2, of which 2 were waited for; matrix products, arithmetic and copies ran while one was open for 4% of the time, Pallas kernels for 0%

commit v1 on v0

--- a/solution.py
+++ b/solution.py
@@ -51,7 +51,9 @@
         grouped = utility.reshape(market_list, nest_count, slot_count, draws_here)
         inner_sum = jnp.sum(grouped, axis=2)
         inclusive_value = jnp.exp(nest_param[None, :, None] * jnp.log(inner_sum))
-        totals = lax.psum(jnp.sum(inclusive_value, axis=1), "nest")
+        part = jnp.sum(inclusive_value, axis=1)
+        parts = lax.all_gather(part, "nest", axis=0, tiled=False)
+        totals = parts.sum(axis=0)
         nest_ratio = inclusive_value / (inner_sum * (1.0 + totals)[:, None, :])
         share_terms = jnp.sum(grouped * nest_ratio[:, :, None, :], axis=3).reshape(
             market_list, columns

time: 172 us -> 161 us (0.936)
  blocking collectives: 61.8 us -> 51.5 us
    psum x3 -> x0, blocking collectives: 17.4 us -> none  [shards(): totals = lax.psum(jnp.sum(inclusive_value, axis=1), 'nest')]
    all_gather x0 -> x3, blocking collectives: none -> 9.76 us  [shards(): parts = lax.all_gather(part, 'nest', axis=0, tiled=False)]
    psum x3, blocking collectives: 44.3 us -> 41.7 us  [shards(): slot_share = lax.psum(share_terms, 'draw') / total_draws]
where the time goes in v1:
time: 161 us
  other arithmetic  61.2 us (38%)
  blocking collectives  51.5 us (32%)
  waiting for transfers between devices  23.1 us (14%)
  starting transfers between devices  8.92 us (6%)
  local copies, waits for them, and re-layouts  8.63 us (5%)
  matrix products  6.48 us (4%)
    psum x3, blocking collectives, shards(): slot_share = lax.psum(share_terms, 'draw') / total_draws  41.7 us
    all_to_all x1, waiting for transfers between devices, shards(): lax.all_to_all(features, 'mkt', split_axis=2, concat_axis=1, tiled=True)  22 us
    mul x3, other arithmetic, shards(): grouped * nest_ratio[:, :, None, :]  20.1 us
    mul x2, other arithmetic, shards(): live_flag[None, :, None]  13.6 us
    reduce_sum x3, other arithmetic, shards(): jnp.sum(grouped * nest_ratio[:, :, None, :], axis=3)  13.4 us
    reduce_sum x3, other arithmetic, shards(): inner_sum = jnp.sum(grouped, axis=2)  11 us
    all_gather x3, blocking collectives, shards(): parts = lax.all_gather(part, 'nest', axis=0, tiled=False)  9.76 us
    dot_general x1, matrix products, shards(): jnp.einsum('dve,dvb->deb', slot_features, taste_matrix, preferred_element...  6.48 us
  transfers between devices with their start and end apart: 2, of which 2 were waited for; matrix products, arithmetic and copies ran while one was open for 4% of the time, Pallas kernels for 0%

profile of v1, /device:TPU:1, one launch (start us, length us, event | category | flops | bytes accessed | tf_op | source)
XLA Modules:
  0.0 160.6 jit_solution(1288049078247704146)
XLA Ops:
  0.7 1.6 copy.37
  2.2 5.4 %all-to-all-start = ((f32[128,4,32]{0,2,1:T(8,128)}), f32[128,4,32]{0,2,1:T(8,128)S(1)}, u32[]{:S(2)}, u32[]{:S(2)}) async-start(f32[128,4,32]{0,2,1:T(8,128)} %bitcast), calls=%async_computation | async-start | bytes 131072 | tf_op jit(solution)/shard_map/all_to_all | solution.py:17
  7.7 0.7 broadcast_in_dim.85
  8.5 2.7 %copy.40 = bf16[32,128,128]{1,0,2:T(8,128)(2,1)} copy(bf16[32,128,128]{2,1,0:T(8,128)(2,1)} %param.6) | data formatting | bytes 2097152 | tf_op args[0]
  11.2 1.1 all-to-all-done
  12.3 3.5 %all-to-all-start.1 = ((bf16[32,128,128]{1,0,2:T(8,128)(2,1)}), bf16[32,128,128]{1,0,2:T(8,128)(2,1)S(1)}, u32[]{:S(2)}, u32[]{:S(2)}) async-start(bf16[32,128,128]{1,0,2:T(8,128)(2,1)} %copy.40), calls=%async_computation.1 | async-start | bytes 2097152 | tf_op jit(solution)/shard_map/all_to_all | solution.py:16
  15.8 0.7 broadcast_maximum_fusion
  16.5 0.7 broadcast_compare_fusion
  17.5 1.1 gather_fusion
  19.1 22.0 %all-to-all-done.1 = bf16[32,128,128]{1,0,2:T(8,128)(2,1)S(1)} async-done(((bf16[32,128,128]{1,0,2:T(8,128)(2,1)}), bf16[32,128,128]{1,0,2:T(8,128)(2,1)S(1)}, u32[]{:S(2)}, u32[]{:S(2)}) %all-to-all-start.1) | async-done | bytes 1048608 | tf_op jit(solution)/shard_map/all_to_all | solution.py:16
  41.0 6.5 %exponential_multiply_fusion.2 = (f32[32,384,128]{2,1,0:T(8,128)}, f32[32,384,128]{2,1,0:T(8,128)}) fusion(f32[384]{0:T(512)S(1)} %reshape.115, f32[32,384]{1,0:T(8,128)S(1)} %copy.39, f32[384]{0:T(512)S(1)} %convert_element_type.20, bf16[32,32,128]{2,1,0:T(8,128)(2,1)S(1)} %copy-done.1, f32[32]{0:T(128)S(1)} %copy-done.2, ...), kind=kOutput, calls=%fused_computation.6 | convolution fusion | flops 509214720 | bytes 13947904 | tf_op jit(solution)/shard_map/dve,dvb->deb/dot_general | solution.py:43
  47.5 3.7 %reduce_sum.118 = f32[32,8,128]{2,1,0:T(8,128)S(1)} reduce(f32[32,8,48,128]{3,2,1,0:T(8,128)} %bitcast.65, f32[]{:T(128)} %constant.28.clone.1), dimensions={2}, to_apply=%region_1.2 | reduce | flops 1540096 | bytes 6422532 | tf_op jit(solution)/shard_map/reduce_sum | solution.py:52
  51.3 3.3 %all-gather = f32[64,128]{1,0:T(8,128)S(1)} all-gather(f32[32,128]{1,0:T(8,128)S(1)} %fusion.27), channel_id=2, replica_groups=mesh['mkt'=4,'draw'=4,'nest'=2] {'nest'}, dimensions={0}, use_global_device_ids=true | all-gather | bytes 49152 | tf_op jit(solution)/shard_map/all_gather | solution.py:55
  54.7 6.2 %bitcast_multiply_fusion.2 = f32[32,384,128]{2,1,0:T(8,128)} fusion(f32[32,384,128]{2,1,0:T(8,128)} %get-tuple-element.12, f32[32,8,128]{2,1,0:T(8,128)S(1)} %multiply_divide_fusion.2), kind=kLoop, calls=%fused_computation.3 | loop fusion | flops 1572864 | bytes 12713984 | tf_op jit(solution)/shard_map/mul | solution.py:58
  60.9 4.5 %reduce_sum.121 = f32[32,384]{1,0:T(8,128)S(1)} reduce(f32[32,384,128]{2,1,0:T(8,128)} %bitcast_multiply_fusion.2, f32[]{:T(128)} %constant.28.clone.1), dimensions={2}, to_apply=%region_4.5 | reduce | flops 1560576 | bytes 6340612 | tf_op jit(solution)/shard_map/reduce_sum | solution.py:58
  65.5 14.5 %psum.21 = f32[32,384]{0,1:T(8,128)S(1)} all-reduce(f32[32,384]{0,1:T(8,128)S(1)} %copy.44), channel_id=1, replica_groups=mesh['mkt'=4,'draw'=4,'nest'=2] {'draw'}, use_global_device_ids=true, to_apply=%region_5.6 | all-reduce | flops 12288 | bytes 98304 | tf_op jit(solution)/shard_map/psum | solution.py:61
  80.3 6.8 %exponential_multiply_fusion.1 = f32[32,384,128]{2,1,0:T(8,128)} fusion(f32[32,384,128]{2,1,0:T(8,128)} %get-tuple-element.13, f32[32,384]{1,0:T(8,128)S(1)} %copy.45, f32[384]{0:T(512)S(1)} %reshape.115, f32[384]{0:T(512)S(1)} %convert_element_type.20), kind=kLoop, calls=%fused_computation.5 | loop fusion | flops 4718592 | bytes 12635136 | tf_op jit(solution)/shard_map/mul | solution.py:48
  87.1 3.7 %reduce_sum.122 = f32[32,8,128]{2,1,0:T(8,128)S(1)} reduce(f32[32,8,48,128]{3,2,1,0:T(8,128)} %bitcast.66, f32[]{:T(128)} %constant.28.clone.1), dimensions={2}, to_apply=%region_6.7 | reduce | flops 1540096 | bytes 6422532 | tf_op jit(solution)/shard_map/reduce_sum | solution.py:52
  90.9 3.3 %all-gather.1 = f32[64,128]{1,0:T(8,128)S(1)} all-gather(f32[32,128]{1,0:T(8,128)S(1)} %fusion.26), channel_id=3, replica_groups=mesh['mkt'=4,'draw'=4,'nest'=2] {'nest'}, dimensions={0}, use_global_device_ids=true | all-gather | bytes 49152 | tf_op jit(solution)/shard_map/all_gather | solution.py:55
  94.3 6.9 %bitcast_multiply_fusion.1 = f32[32,384,128]{2,1,0:T(8,128)} fusion(f32[32,8,128]{2,1,0:T(8,128)S(1)} %multiply_divide_fusion.1, f32[384]{0:T(512)S(1)} %reshape.115, f32[32,384,128]{2,1,0:T(8,128)} %get-tuple-element.13, f32[32,384]{1,0:T(8,128)S(1)} %copy.45, f32[384]{0:T(512)S(1)} %convert_element_type.20), kind=kLoop, calls=%fused_computation.2 | loop fusion | flops 6291456 | bytes 12766208 | tf_op jit(solution)/shard_map/mul | solution.py:58
  101.2 4.5 %reduce_sum.125 = f32[32,384]{1,0:T(8,128)S(1)} reduce(f32[32,384,128]{2,1,0:T(8,128)} %bitcast_multiply_fusion.1, f32[]{:T(128)} %constant.28.clone.1), dimensions={2}, to_apply=%region_9.10 | reduce | flops 1560576 | bytes 6340612 | tf_op jit(solution)/shard_map/reduce_sum | solution.py:58
  105.8 13.7 %psum.22 = f32[32,384]{0,1:T(8,128)S(1)} all-reduce(f32[32,384]{0,1:T(8,128)S(1)} %copy.46), channel_id=1, replica_groups=mesh['mkt'=4,'draw'=4,'nest'=2] {'draw'}, use_global_device_ids=true, to_apply=%region_10.11 | all-reduce | flops 12288 | bytes 98304 | tf_op jit(solution)/shard_map/psum | solution.py:61
  119.5 0.2 fusion.21
  119.9 6.8 %exponential_multiply_fusion = f32[32,384,128]{2,1,0:T(8,128)} fusion(f32[32,384,128]{2,1,0:T(8,128)} %get-tuple-element.13, f32[32,384]{1,0:T(8,128)S(1)} %copy.47, f32[384]{0:T(512)S(1)} %reshape.115, f32[384]{0:T(512)S(1)} %convert_element_type.20), kind=kLoop, calls=%fused_computation.4 | loop fusion | flops 4718592 | bytes 12635136 | tf_op jit(solution)/shard_map/mul | solution.py:48
  126.7 3.7 %reduce_sum.126 = f32[32,8,128]{2,1,0:T(8,128)S(1)} reduce(f32[32,8,48,128]{3,2,1,0:T(8,128)} %bitcast.67, f32[]{:T(128)} %constant.28.clone.1), dimensions={2}, to_apply=%region_11.12 | reduce | flops 1540096 | bytes 6422532 | tf_op jit(solution)/shard_map/reduce_sum | solution.py:52
  130.4 3.3 %all-gather.2 = f32[64,128]{1,0:T(8,128)S(1)} all-gather(f32[32,128]{1,0:T(8,128)S(1)} %fusion.25), channel_id=4, replica_groups=mesh['mkt'=4,'draw'=4,'nest'=2] {'nest'}, dimensions={0}, use_global_device_ids=true | all-gather | bytes 49152 | tf_op jit(solution)/shard_map/all_gather | solution.py:55
  133.8 6.9 %bitcast_multiply_fusion = f32[32,384,128]{2,1,0:T(8,128)} fusion(f32[32,8,128]{2,1,0:T(8,128)S(1)} %multiply_divide_fusion, f32[384]{0:T(512)S(1)} %reshape.115, f32[32,384,128]{2,1,0:T(8,128)} %get-tuple-element.13, f32[32,384]{1,0:T(8,128)S(1)} %copy.47, f32[384]{0:T(512)S(1)} %convert_element_type.20), kind=kLoop, calls=%fused_computation.1 | loop fusion | flops 6291456 | bytes 12766208 | tf_op jit(solution)/shard_map/mul | solution.py:58
  140.8 4.5 %reduce_sum.129 = f32[32,384]{1,0:T(8,128)S(1)} reduce(f32[32,384,128]{2,1,0:T(8,128)} %bitcast_multiply_fusion, f32[]{:T(128)} %constant.28.clone.1), dimensions={2}, to_apply=%region_14.15 | reduce | flops 1560576 | bytes 6340612 | tf_op jit(solution)/shard_map/reduce_sum | solution.py:58
  145.4 13.5 %psum.23 = f32[32,384]{0,1:T(8,128)S(1)} all-reduce(f32[32,384]{0,1:T(8,128)S(1)} %copy.48), channel_id=1, replica_groups=mesh['mkt'=4,'draw'=4,'nest'=2] {'draw'}, use_global_device_ids=true, to_apply=%region_15.16 | all-reduce | flops 12288 | bytes 98304 | tf_op jit(solution)/shard_map/psum | solution.py:61
  158.9 0.2 broadcast_multiply_fusion
  159.1 0.7 copy.49
  159.9 0.7 copy.50
  (36 shorter events, 2.3 us)
Async XLA Ops:
  0.6 40.4 %copy-start.1 = (bf16[32,32,128]{2,1,0:T(8,128)(2,1)S(1)}, bf16[32,32,128]{2,1,0:T(8,128)(2,1)}, u32[]{:S(2)}) copy-start(bf16[32,32,128]{2,1,0:T(8,128)(2,1)} %param.7) | copy-start | bytes 786436
  0.6 40.4 %copy-start.2 = (f32[32]{0:T(128)S(1)}, f32[32]{0:T(128)}, u32[]{:S(2)}) copy-start(f32[32]{0:T(128)} %param.8) | copy-start | bytes 388
  2.2 10.0 %all-to-all-start = ((f32[128,4,32]{0,2,1:T(8,128)}), f32[128,4,32]{0,2,1:T(8,128)S(1)}, u32[]{:S(2)}, u32[]{:S(2)}) async-start(f32[128,4,32]{0,2,1:T(8,128)} %bitcast), calls=%async_computation | async-start | bytes 131072 | tf_op jit(solution)/shard_map/all_to_all | solution.py:17
  12.3 28.8 %all-to-all-start.1 = ((bf16[32,128,128]{1,0,2:T(8,128)(2,1)}), bf16[32,128,128]{1,0,2:T(8,128)(2,1)S(1)}, u32[]{:S(2)}, u32[]{:S(2)}) async-start(bf16[32,128,128]{1,0,2:T(8,128)(2,1)} %copy.40), calls=%async_computation.1 | async-start | bytes 2097152 | tf_op jit(solution)/shard_map/all_to_all | solution.py:16
  47.5 3.7 %copy-start = (f32[8]{0:T(128)S(1)}, f32[8]{0:T(128)}, u32[]{:S(2)}) copy-start(f32[8]{0:T(128)} %param.9) | copy-start | bytes 100
